TPU v7x, 512 devices: a whole 4x8x8 slice. The times are simulated.
512 devices in a mesh: row: 32 (over x_lo, y, core), col: 16 (over z, x_hi).
Axes of the slice: x: 4 (x_hi: 2, x_lo: 2; x = x_hi * 2 + x_lo), y: 8, z: 8, core: 2. Of those that a mesh axis runs over, the one named last changes fastest.
Arguments:
- x_slab: float32 [8192, 4096], P('col', 'row'), may hold values from -5400 to 5400, as said below
- weight_c: float32 [1], replicated, may hold values from 2048 to 16384
Outputs:
- trailing: float32 [4096, 4096], P('row', 'col')
- panels: float32 [4096, 512], P('row')
- inverses: float32 [2, 256, 256], replicated
- frobenius: float32 [1], replicated
Inputs may be any that keep to these rules, and one draw needn't show every extreme that they name: `x_slab`: real-valued entries.
All inputs are finite; a program needn't handle non-finite values.
Results may differ from a plain program's by a relative error of at most 0.00015.
Values sent between devices are 32-bit elements; how exact they have to be, the bound alone decides.
A program may use at most 64 MiB of HBM per device.

v0:
```python
import jax
import jax.numpy as jnp
from jax import lax
from jax.sharding import Mesh
from jax.sharding import PartitionSpec as P

PANEL = 256
COL = ("col_0", "col_1")
ROW = ("row_0", "row_1", "row_2")
ROW_COL = ("row_0", "row_1", "row_2", "col_0", "col_1")


HIGH = lax.Precision.HIGHEST


def broadcast(x, axis, root):
    return lax.dynamic_index_in_dim(lax.all_gather(x, axis), root, 0, keepdims=False)


def split_up(x, dim, size):
    dims = x.shape
    blocks = x.reshape(*dims[:dim], size, dims[dim] // size, *dims[dim + 1 :])
    return jnp.moveaxis(blocks, dim, 0)


def summed_on_arrival(x, axis, dim):
    blocks = split_up(x, dim, lax.axis_size(axis))
    arrived = lax.all_to_all(blocks, axis, split_axis=0, concat_axis=0, tiled=True)
    return arrived.sum(axis=0)


def rows_for(lines, size):
    spare = -len(lines) % size
    return jnp.pad(lines, [(0, spare)] + [(0, 0)] * (lines.ndim - 1))


def joined_along(blocks, dim):
    blocks = jnp.moveaxis(blocks, 0, dim)
    dims = blocks.shape
    return blocks.reshape(*dims[:dim], dims[dim] * dims[dim + 1], *dims[dim + 2 :])


def from_everyone(x, axis):
    size = lax.axis_size(axis)
    return lax.all_to_all(jnp.broadcast_to(x[None], (size, *x.shape)), axis, 0, 0, tiled=True)


def collect(x, axis, dim):
    return joined_along(from_everyone(x, axis), dim)


def sum_by_parts(x, axes):
    lines = x.reshape(-1, x.shape[-1])
    own = summed_on_arrival(rows_for(lines, lax.axis_size(axes)), axes, 0)
    whole = collect(own, axes, 0)
    return whole[: len(lines)].reshape(x.shape)


def by_axis(x, axes):
    for axis in axes:
        x = lax.psum(x, axis)
    return x


def nested_sum(x, axes):
    own = summed_on_arrival(rows_for(x, lax.axis_size(axes)), axes, 0)
    whole = collect(own, axes, 0)
    return whole[: len(x)].reshape(x.shape)


def packed_total(arrays, axis):
    ends = [0]
    for a in arrays:
        ends.append(ends[-1] + a.size)
    subtotal = nested_sum(jnp.concatenate([a.ravel() for a in arrays]), axis)
    return tuple((subtotal[b:e].reshape(a.shape) for a, b, e in zip(arrays, ends, ends[1:])))


def product(left, right):
    return jnp.dot(left, right, preferred_element_type=jnp.float32, precision=HIGH)


def invert_lower(block):
    factor = jnp.linalg.cholesky(block)
    identity = jnp.eye(block.shape[0], dtype=block.dtype)
    return lax.linalg.triangular_solve(factor, identity, left_side=True, lower=True)


def lower_panel(column, inverse, start, row_ids, panel_size):
    values = product(column, inverse.T)
    targets = start + jnp.arange(panel_size, dtype=jnp.int32)
    return jnp.where(row_ids[:, None] >= targets[None, :], values, jnp.zeros_like(values))


def panel_column(matrix, number, panel_size, tile_cols):
    owner = number * panel_size // tile_cols
    return broadcast(matrix, COL, owner)


def pick_rows(values, start, row_ids, panel_size):
    targets = start + jnp.arange(panel_size, dtype=jnp.int32)
    selector = (targets[:, None] == row_ids[None, :]).astype(jnp.float32)
    return product(selector, values)


def diagonal_block(column, start, row_ids, panel_size):
    return sum_by_parts(pick_rows(column, start, row_ids, panel_size), ROW)


def on_device(x_slab, weight_c):
    local_cols = x_slab.shape[1]
    width = local_cols * lax.axis_size(ROW)
    tile_cols = width // lax.axis_size(COL)
    panel_size = PANEL
    row_ids = lax.axis_index(ROW) * local_cols + jnp.arange(local_cols, dtype=jnp.int32)
    col_ids = lax.axis_index(COL) * tile_cols + jnp.arange(tile_cols, dtype=jnp.int32)
    squares = by_axis(jnp.sum(x_slab * x_slab), ROW_COL)
    factor_c = weight_c[0] / squares
    partial_value = lax.dot_general(
        x_slab,
        lax.all_gather(x_slab, ROW, axis=1, tiled=True),
        (((0,), (0,)), ((), ())),
        precision=HIGH,
        preferred_element_type=jnp.float32,
    )
    block = summed_on_arrival(partial_value, COL, 1)
    gram = block * factor_c + (row_ids[:, None] == col_ids[None, :]).astype(jnp.float32)
    column_one = panel_column(gram, 0, panel_size, tile_cols)
    column_two = panel_column(gram, 1, panel_size, tile_cols)
    inverse_one = invert_lower(diagonal_block(column_one, 0, row_ids, panel_size))
    lower_one = lower_panel(column_one, inverse_one, 0, row_ids, panel_size)
    raw_block, crossing = packed_total(
        (
            pick_rows(column_two, panel_size, row_ids, panel_size),
            pick_rows(lower_one, panel_size, row_ids, panel_size),
        ),
        ROW,
    )
    inverse_two = invert_lower(raw_block - product(crossing, crossing.T))
    lower_two = lower_panel(
        column_two - product(lower_one, crossing.T), inverse_two, panel_size, row_ids, panel_size
    )
    both = jnp.concatenate([lower_one, lower_two], axis=1)
    gathered = lax.all_gather(both, ROW, axis=0, tiled=True)
    mine = lax.dynamic_slice_in_dim(gathered, lax.axis_index(COL) * tile_cols, tile_cols, 0)
    matrix = gram - product(both, mine.T)
    inverses = [inverse_one, inverse_two]
    return (matrix, both, jnp.stack(inverses), jnp.sqrt(squares).reshape(1))


def solution(mesh):
    split = Mesh(mesh.devices.reshape(2, 8, 2, 8, 2), ("row_0", "row_1", "row_2", "col_0", "col_1"))
    in_specs = (P(COL, ROW), P())
    out_specs = (P(ROW, COL), P(ROW, None), P(), P())
    return jax.shard_map(
        on_device, mesh=split, in_specs=in_specs, out_specs=out_specs, check_vma=False
    )
```

profile of v0, /device:TPU:1, one launch (start us, length us, event | category | flops | bytes accessed | tf_op | source)
XLA Modules:
  0.0 573.3 jit_solution(13100792732569455945)
XLA Ops:
  7.9 98.4 %all-gather.4.cloned.1.call-done = f32[512,4096]{1,0:T(8,128)} async-done(((f32[512,128]{1,0:T(8,128)}), f32[512,4096]{1,0:T(8,128)}) %all-gather.4.cloned.1.call-update) | async-done | bytes 8388624 | tf_op jit(solution)/shard_map/all_gather | solution.py:121
  106.3 6.9 %fusion.41 = f32[128,4096]{1,0:T(8,128)S(1)} fusion(f32[512,128]{1,0:T(8,128)} %param.5, f32[512,4096]{1,0:T(8,128)} %all-gather.4.cloned.1.call-done), kind=kOutput, calls=%fused_computation.97 | convolution fusion | flops 3221225472 | bytes 10747904 | tf_op jit(solution)/shard_map/dot_general | solution.py:119
  113.2 1.6 copy.21
  114.8 9.5 %all-to-all-start = ((f32[16,128,256]{2,1,0:T(8,128)}), f32[16,128,256]{2,1,0:T(8,128)S(1)}, u32[]{:S(2)}, u32[]{:S(2)}) async-start(f32[16,128,256]{2,1,0:T(8,128)} %bitcast.100), calls=%async_computation | async-start | bytes 4194304 | tf_op jit(solution)/shard_map/all_to_all | solution.py:28
  125.0 4.4 psum.35
  129.4 15.1 %psum.36 = f32[]{:T(128)} all-reduce(f32[]{:T(128)} %psum.35), channel_id=1, replica_groups=mesh['row_0'=2,'row_1'=8,'row_2'=2,'col_0'=8,'col_1'=2] {'row_1'}, use_global_device_ids=true, to_apply=%region_3.0 | all-reduce | flops 1 | bytes 8 | tf_op jit(solution)/shard_map/psum | solution.py:61
  144.5 6.4 %psum.37 = f32[]{:T(128)} all-reduce(f32[]{:T(128)} %psum.36), channel_id=1, replica_groups=mesh['row_0'=2,'row_1'=8,'row_2'=2,'col_0'=8,'col_1'=2] {'row_2'}, use_global_device_ids=true, to_apply=%region_4.0 | all-reduce | flops 1 | bytes 8 | tf_op jit(solution)/shard_map/psum | solution.py:61
  151.0 28.8 %psum.38 = f32[]{:T(128)} all-reduce(f32[]{:T(128)} %psum.37), channel_id=1, replica_groups=mesh['row_0'=2,'row_1'=8,'row_2'=2,'col_0'=8,'col_1'=2] {'col_0'}, use_global_device_ids=true, to_apply=%region_5.0 | all-reduce | flops 1 | bytes 8 | tf_op jit(solution)/shard_map/psum | solution.py:61
  179.8 5.9 %psum.39 = f32[]{:T(128)} all-reduce(f32[]{:T(128)} %psum.38), channel_id=1, replica_groups=mesh['row_0'=2,'row_1'=8,'row_2'=2,'col_0'=8,'col_1'=2] {'col_1'}, use_global_device_ids=true, to_apply=%region_6.0 | all-reduce | flops 1 | bytes 8 | tf_op jit(solution)/shard_map/psum | solution.py:61
  187.9 90.3 %all-gather.6.cloned.1.call-done = f32[16,128,256]{2,1,0:T(8,128)} async-done(((f32[1,128,256]{2,1,0:T(8,128)}), f32[16,128,256]{2,1,0:T(8,128)}) %all-gather.6.cloned.1.call-update) | async-done | bytes 2097168 | tf_op jit(solution)/shard_map/all_gather | solution.py:17
  279.4 22.4 %all_to_all.30 = f32[32,8,256]{2,1,0:T(8,128)S(1)} all-to-all(f32[32,8,256]{2,1,0:T(8,128)S(1)} %fusion.10), channel_id=1, replica_groups=mesh['row_0'=2,'row_1'=8,'row_2'=2,'col_0'=8,'col_1'=2] {'row_0','row_1'..., dimensions={0} | all-to-all | bytes 524288 | tf_op jit(solution)/shard_map/all_to_all | solution.py:28
  302.5 5.6 all-to-all-start.2
  309.5 10.4 %all-to-all-done.2 = f32[32,8,256]{2,1,0:T(8,128)S(1)} async-done(((f32[32,8,256]{2,1,0:T(8,128)}), f32[32,8,256]{2,1,0:T(8,128)S(1)}, u32[]{:S(2)}, u32[]{:S(2)}) %all-to-all-start.2) | async-done | bytes 262176 | tf_op jit(solution)/shard_map/all_to_all | solution.py:45
  320.1 11.7 %cholesky.130 = f32[128,128]{1,0:T(8,128)S(1)} custom-call(f32[128,128]{1,0:T(8,128)S(1)} %cholesky.194), custom_call_target="Cholesky" | custom-call | tf_op jit(solution)/shard_map/jit(cholesky)/cholesky | solution.py:84
  331.9 9.8 %custom-call.13 = f32[1,128,128]{1,2,0:T(8,128)S(1)} custom-call(f32[1,128,128]{2,1,0:T(8,128)S(1)} %get-tuple-element.51), custom_call_target="InvertDiagBlocksLowerTriangular" | custom-call | tf_op jit(solution)/shard_map/jit(cholesky)/cholesky | solution.py:84
  342.2 11.7 %cholesky.147 = f32[128,128]{1,0:T(8,128)S(1)} custom-call(f32[128,128]{1,0:T(8,128)S(1)} %convolution_subtract_fusion.6), custom_call_target="Cholesky" | custom-call | tf_op jit(solution)/shard_map/jit(cholesky)/cholesky | solution.py:84
  356.0 4.0 while.4
  356.6 1.4 bitcast_dynamic-update-slice_fusion.4
  358.6 1.4 bitcast_dynamic-update-slice_fusion.4
  360.0 19.9 %custom-call.14 = f32[2,128,128]{1,2,0:T(8,128)S(1)} custom-call(f32[2,128,128]{2,1,0:T(8,128)S(1)} %get-tuple-element.20), custom_call_target="InvertDiagBlocksLowerTriangular" | custom-call | tf_op jit(solution)/shard_map/triangular_solve/custom-call.0 | solution.py:86
  383.1 21.0 %all_to_all.31 = f32[32,1,4096]{2,1,0:T(1,128)S(1)} all-to-all(f32[32,1,4096]{2,1,0:T(1,128)S(1)} %all_to_all.22), channel_id=1, replica_groups=mesh['row_0'=2,'row_1'=8,'row_2'=2,'col_0'=8,'col_1'=2] {'row_0','row_1'..., dimensions={0} | all-to-all | bytes 1048576 | tf_op jit(solution)/shard_map/all_to_all | solution.py:28
  405.7 5.6 all-to-all-start.4
  411.4 16.7 %all-to-all-done.4 = f32[32,1,4096]{2,1,0:T(1,128)S(1)} async-done(((f32[32,1,4096]{2,1,0:T(1,128)}), f32[32,1,4096]{2,1,0:T(1,128)S(1)}, u32[]{:S(2)}, u32[]{:S(2)}) %all-to-all-start.4) | async-done | bytes 524320 | tf_op jit(solution)/shard_map/all_to_all | solution.py:45
  430.2 11.7 %cholesky.164 = f32[128,128]{1,0:T(8,128)S(1)} custom-call(f32[128,128]{1,0:T(8,128)S(1)} %cholesky.197), custom_call_target="Cholesky" | custom-call | tf_op jit(solution)/shard_map/jit(cholesky)/cholesky | solution.py:84
  442.0 9.8 %custom-call.15 = f32[1,128,128]{1,2,0:T(8,128)S(1)} custom-call(f32[1,128,128]{2,1,0:T(8,128)S(1)} %get-tuple-element.47), custom_call_target="InvertDiagBlocksLowerTriangular" | custom-call | tf_op jit(solution)/shard_map/jit(cholesky)/cholesky | solution.py:84
  452.3 11.9 %cholesky.181 = f32[128,128]{1,0:T(8,128)S(1)} custom-call(f32[128,128]{1,0:T(8,128)S(1)} %convolution_subtract_fusion.5), custom_call_target="Cholesky" | custom-call | tf_op jit(solution)/shard_map/jit(cholesky)/cholesky | solution.py:84
  466.9 4.0 while.5
  467.5 1.4 bitcast_dynamic-update-slice_fusion.5
  469.5 1.4 bitcast_dynamic-update-slice_fusion.5
  470.9 19.7 %custom-call.16 = f32[2,128,128]{1,2,0:T(8,128)S(1)} custom-call(f32[2,128,128]{2,1,0:T(8,128)S(1)} %get-tuple-element.21), custom_call_target="InvertDiagBlocksLowerTriangular" | custom-call | tf_op jit(solution)/shard_map/triangular_solve/custom-call.0 | solution.py:86
  495.5 67.3 %all-gather.8.cloned.1.call-done = f32[4096,512]{1,0:T(8,128)} async-done(((f32[128,512]{1,0:T(8,128)}), f32[4096,512]{1,0:T(8,128)}) %all-gather.8.cloned.1.call-update) | async-done | bytes 8388624 | tf_op jit(solution)/shard_map/all_gather | solution.py:144
  562.8 2.4 convolution_subtract_fusion.1
  (81 shorter events, 22.5 us)
Async XLA Ops:
  7.2 99.1 %all-gather.4.cloned.1.call-start = ((), (), s32[]{:S(2)}) async-start(), calls=%async_computation.5 | async-start | bytes 8650752 | tf_op jit(solution)/shard_map/all_gather | solution.py:121
  114.8 9.6 %copy-start.1 = (f32[512,128]{1,0:T(8,128)S(1)}, f32[512,128]{1,0:T(8,128)}, u32[]{:S(2)}) copy-start(f32[512,128]{1,0:T(8,128)} %param.5) | copy-start | bytes 786436
  114.8 72.2 %all-to-all-start = ((f32[16,128,256]{2,1,0:T(8,128)}), f32[16,128,256]{2,1,0:T(8,128)S(1)}, u32[]{:S(2)}, u32[]{:S(2)}) async-start(f32[16,128,256]{2,1,0:T(8,128)} %bitcast.100), calls=%async_computation | async-start | bytes 4194304 | tf_op jit(solution)/shard_map/all_to_all | solution.py:28
  124.3 153.9 %all-gather.6.cloned.1.call-start = ((), (), s32[]{:S(2)}) async-start(), calls=%async_computation.6 | async-start | bytes 2228224 | tf_op jit(solution)/shard_map/all_gather | solution.py:17
  302.5 17.4 %all-to-all-start.2 = ((f32[32,8,256]{2,1,0:T(8,128)}), f32[32,8,256]{2,1,0:T(8,128)S(1)}, u32[]{:S(2)}, u32[]{:S(2)}) async-start(f32[32,8,256]{2,1,0:T(8,128)} %broadcast_in_dim.4), calls=%async_computation.2 | async-start | bytes 524288 | tf_op jit(solution)/shard_map/all_to_all | solution.py:45
  405.7 22.3 %all-to-all-start.4 = ((f32[32,1,4096]{2,1,0:T(1,128)}), f32[32,1,4096]{2,1,0:T(1,128)S(1)}, u32[]{:S(2)}, u32[]{:S(2)}) async-start(f32[32,1,4096]{2,1,0:T(1,128)} %broadcast_in_dim.5), calls=%async_computation.4 | async-start | bytes 1048576 | tf_op jit(solution)/shard_map/all_to_all | solution.py:45
  411.3 151.5 %all-gather.8.cloned.1.call-start = ((), (), s32[]{:S(2)}) async-start(), calls=%async_computation.7 | async-start | bytes 8650752 | tf_op jit(solution)/shard_map/all_gather | solution.py:144
  494.0 68.9 %copy-start = (f32[128,512]{1,0:T(8,128)S(1)}, f32[128,512]{1,0:T(8,128)}, u32[]{:S(2)}) copy-start(f32[128,512]{1,0:T(8,128)} %pad_maximum_fusion.4) | copy-start | bytes 786436
Sparse Core Ops, SparseCore 0:
  10.0 96.2 all-gather.3
  188.0 90.1 all-gather.5
  494.1 68.6 all-gather.7
where the time goes:
time: 584 us; the launch traced here: 573 us
  waiting for transfers between devices  284 us (49%)
  other arithmetic  112 us (19%)
  blocking collectives  104 us (18%)
  starting transfers between devices  20.9 us (4%)
  between operations  20.3 us (3%)
  matrix products  18.1 us (3%)
  local copies, waits for them, and re-layouts  14.1 us (2%)
    all_gather x1, waiting for transfers between devices, on_device(): lax.all_gather(x_slab, ROW, axis=1, tiled=True)  98.4 us
    all_gather x1, waiting for transfers between devices, broadcast(): lax.all_gather(x, axis)  90.3 us
    another operation x13, other arithmetic, invert_lower(): factor = jnp.linalg.cholesky(block)  68.8 us
    all_gather x1, waiting for transfers between devices, on_device(): gathered = lax.all_gather(both, ROW, axis=0, tiled=True)  67.3 us
    psum x5, blocking collectives, by_axis(): x = lax.psum(x, axis)  60.7 us
    all_to_all x2, blocking collectives, summed_on_arrival(): lax.all_to_all(blocks, axis, split_axis=0, concat_axis=0, tiled=True)  43.3 us
    another operation x5, other arithmetic, invert_lower(): lax.linalg.triangular_solve(factor, identity, left_side=True, lower=True)  39.6 us
    all_to_all x2, waiting for transfers between devices, from_everyone(): lax.all_to_all(jnp.broadcast_to(x[None], (size, *x.shape)), axis, 0, 0, t...  27.1 us
  transfers between devices with their start and end apart: 6, of which 5 were waited for; matrix products, arithmetic and copies ran while one was open for 0% of the time, Pallas kernels for 0%

commit v1 on v0

v1 whole, which is shorter than its diff:
```python
import functools

import jax
import jax.numpy as jnp
from jax import lax
from jax.experimental import pallas as pl
from jax.experimental.pallas import tpu as pltpu
from jax.sharding import Mesh
from jax.sharding import PartitionSpec as P

PANEL = 256
AXES = ("x", "y", "core", "z", "h")
ROW = ("x", "y", "core")
COL = ("z", "h")
HIGH = lax.Precision.HIGHEST
F32 = jnp.float32


def rem(a, n):
    return lax.rem(a + n, n)


def place():
    x, y, k = lax.axis_index("x"), lax.axis_index("y"), lax.axis_index("core")
    z, h = lax.axis_index("z"), lax.axis_index("h")
    return x, y, k, z, h


def gram_kernel(
    x_ref, tile_ref, ga_ref, gb_ref, d_ref, sq_ref,
    xb, other, lhs, prod, stage, landed, mine, ring, parts, flip, pile, turned, half, sq2,
    s_ring, r_ring, s_core, r_core, s_rs, r_rs, s_pl, r_pl, s_ag, r_ag, s_a2a, r_a2a, s_t, r_t,
):
    x, y, k, z, h = place()
    a = x * 8 + y
    b = z * 2 + h
    gap = rem(b - a, 16)

    def at_a(i):
        return (lax.div(i, 8), lax.rem(i, 8), k, z, h)

    def at_b(i):
        return (x, y, k, lax.div(i, 2), lax.rem(i, 2))

    partner = (x, y, 1 - k, z, h)
    mirror = (lax.div(b, 8), lax.rem(b, 8), k, lax.div(a, 2), lax.rem(a, 2))

    def copy(src, dst, ssem, rsem, dev):
        return pltpu.make_async_remote_copy(
            src_ref=src, dst_ref=dst, send_sem=ssem, recv_sem=rsem,
            device_id=dev, device_id_type=pl.DeviceIdType.MESH,
        )

    barrier = pltpu.get_barrier_semaphore()

    def signal(dev):
        pl.semaphore_signal(barrier, inc=1, device_id=dev, device_id_type=pl.DeviceIdType.MESH)

    @pl.loop(1, 16)
    def _(i):
        signal(at_a(lax.rem(a + i, 16)))
        signal(at_b(lax.rem(b + i, 16)))

    signal(partner)

    @pl.when(a != b)
    def _():
        signal(mirror)

    @pl.when(a != b)
    def _():
        pl.semaphore_wait(barrier, 32)

    @pl.when(a == b)
    def _():
        pl.semaphore_wait(barrier, 31)

    sgn = 1 - 2 * k

    def slot(xx, dy):
        return xx * 8 + rem(y + dy + 8, 8)

    def pass_on(src, who, to, n):
        return copy(src, xb.at[who], s_ring.at[n], r_ring.at[who], to)

    def y_at(dy):
        return (x, rem(y + dy + 8, 8), k, z, h)

    across = (1 - x, y, k, z, h)
    sent = []

    def go(who, to, src=None):
        c = pass_on(xb.at[who] if src is None else src, who, to, len(sent))
        c.start()
        sent.append(c)

    def arrive(who):
        pass_on(xb.at[who], who, across, 0).wait_recv()

    go(a, y_at(1), x_ref)
    go(a, y_at(-1), x_ref)
    go(a, across, x_ref)
    to_core = copy(x_ref, other, s_core.at[0], r_core.at[0], partner)
    to_core.start()
    xb[a] = x_ref[...]
    arrive(slot(x, -1))
    go(slot(x, -1), y_at(1))
    go(slot(x, -1), across)
    arrive(slot(x, 1))
    go(slot(x, 1), y_at(-1))
    go(slot(x, 1), across)
    to_core.wait_recv()
    lhs[:, pl.ds(pl.multiple_of(k * 128, 128), 128)] = x_ref[...]
    lhs[:, pl.ds(pl.multiple_of((1 - k) * 128, 128), 128)] = other[...]
    arrive(slot(1 - x, 0))
    arrive(slot(x, -2))
    go(slot(x, -2), y_at(1))
    arrive(slot(x, 2))
    go(slot(x, 2), y_at(-1))
    arrive(slot(1 - x, -1))
    go(slot(1 - x, -1), y_at(1))
    arrive(slot(1 - x, 1))
    go(slot(1 - x, 1), y_at(-1))
    arrive(slot(x, -3))
    arrive(slot(x, 3))
    go(slot(x, -3 * sgn), y_at(sgn))
    arrive(slot(1 - x, -2))
    go(slot(1 - x, -2), y_at(1))
    arrive(slot(1 - x, 2))
    go(slot(1 - x, 2), y_at(-1))
    arrive(slot(1 - x, -3))
    arrive(slot(1 - x, 3))
    go(slot(1 - x, -3 * sgn), y_at(sgn))
    arrive(slot(x, 4))
    arrive(slot(1 - x, 4))

    def multiply(i, total):
        blk = xb[i]
        prod[i] = lax.dot_general(
            blk, lhs[...], (((0,), (0,)), ((), ())), precision=HIGH, preferred_element_type=F32
        )
        return total + jnp.sum((blk * blk).reshape(64, 8, 128), axis=0)

    total = lax.fori_loop(0, 16, multiply, jnp.zeros((8, 128), F32))
    for i in range(16):
        stage[i, 0:16, :] = prod[i // 8, (i % 8) * 16 : (i % 8) * 16 + 16, :]
        stage[i, 16:24, 0:128] = total
        stage[i, 16:24, 128:256] = jnp.zeros((8, 128), F32)

    def rs(i):
        to = lax.rem(b + i, 16)
        return copy(stage.at[to], landed.at[b], s_rs.at[i], r_rs.at[b], at_b(to))

    def rs_from(i):
        who = lax.rem(b + i, 16)
        return copy(stage.at[who], landed.at[who], s_rs.at[i], r_rs.at[who], at_b(who))

    @pl.loop(1, 16)
    def _(i):
        rs(i).start()

    landed[b] = stage[b]

    @pl.loop(1, 16)
    def _(i):
        rs_from(i).wait_recv()

    red = landed[0]
    for i in range(1, 16):
        red = red + landed[i]
    mine[0:16, :] = red[0:16]
    sq_ref[...] = red[16:24]

    def spread(i):
        to = lax.rem(a + i, 16)
        rows = pl.ds(pl.multiple_of(16 + 16 * a, 16), 16)
        return copy(mine.at[0:16], mine.at[rows], s_pl.at[i], r_pl.at[a], at_a(to))

    @pl.when(a < 2)
    def _():
        @pl.loop(1, 16)
        def _(i):
            spread(i).start()

        mine[pl.ds(pl.multiple_of(16 + 16 * a, 16), 16), :] = red[0:16]

    for i in range(2):

        @pl.when(a != i)
        def _():
            copy(mine.at[0:16], mine.at[16 + 16 * i : 32 + 16 * i], s_pl.at[0], r_pl.at[i], across).wait_recv()

    def ag(i):
        to = lax.rem(b + i, 16)
        return copy(mine, ring.at[b], s_ag.at[i], r_ag.at[b], at_b(to))

    def ag_from(i):
        who = lax.rem(b + i, 16)
        return copy(mine, ring.at[who], s_ag.at[i], r_ag.at[who], at_b(who))

    @pl.loop(1, 16)
    def _(i):
        ag(i).start()

    ring[b] = mine[...]

    def tile(d):
        to = lax.rem(a + d, 16)
        return to, copy(prod.at[to], pile.at[b], s_a2a.at[d], r_a2a.at[b], at_b(to))

    @pl.loop(0, 9)
    def _(d):
        to, c = tile(d)

        @pl.when(to != b)
        def _():
            c.start()

    @pl.loop(1, 16)
    def _(i):
        ag_from(i).wait_recv()

    for i in range(16):
        r = (i % 8) * 16
        for j in range(3):
            parts[k, j, i // 8, r : r + 16, :] = ring[i, 16 * j : 16 * j + 16, :]
    swap = copy(parts.at[k], parts.at[k], s_core.at[1], r_core.at[1], partner)
    swap_in = copy(parts.at[1 - k], parts.at[1 - k], s_core.at[1], r_core.at[1], partner)
    swap.start()
    swap_sq = copy(sq_ref, sq2, s_core.at[2], r_core.at[2], partner)
    swap_sq.start()
    send_flip = copy(parts.at[k, 0], flip.at[k], s_t.at[0], r_t.at[0], mirror)

    @pl.when(a != b)
    def _():
        send_flip.start()

    @pl.when(a == b)
    def _():
        flip[k] = parts[k, 0]

    swap_in.wait_recv()
    swap_sq.wait()
    sq_ref[...] = sq_ref[...] + sq2[...]
    for kk in range(2):
        for i in range(2):
            r = i * 256 + kk * 128
            ga_ref[r : r + 128, :] = parts[kk, 0, i]
            for j in range(2):
                d_ref[r : r + 128, 256 * j : 256 * j + 256] = parts[kk, 1 + j, i]

    @pl.when(a != b)
    def _():
        send_flip.wait_recv()

    flop = copy(flip.at[k], flip.at[k], s_core.at[3], r_core.at[3], partner)
    flop_in = copy(flip.at[1 - k], flip.at[1 - k], s_core.at[3], r_core.at[3], partner)
    flop.start()

    send_turn = copy(turned, half, s_t.at[1], r_t.at[1], mirror)
    trade = copy(
        turned.at[:, pl.ds(pl.multiple_of((1 - k) * 128, 128), 128)],
        half.at[:, 0:128],
        s_core.at[4], r_core.at[4], partner,
    )

    @pl.when(gap <= 8)
    def _():
        pile[b] = prod[b]

        @pl.loop(1, 16)
        def _(i):
            who = lax.rem(b + i, 16)
            copy(prod.at[who], pile.at[who], s_a2a.at[0], r_a2a.at[who], at_b(who)).wait_recv()

        total_tile = pile[0]
        for i in range(1, 16):
            total_tile = total_tile + pile[i]
        turned[...] = total_tile
        trade.start()

        @pl.when((gap >= 1) & (gap <= 7))
        def _():
            send_turn.start()

        own = turned[:, pl.ds(pl.multiple_of(k * 128, 128), 128)]
        tile_ref[:, pl.ds(pl.multiple_of(k * 128, 128), 128)] = own.T
        trade.wait_recv()
        tile_ref[:, pl.ds(pl.multiple_of((1 - k) * 128, 128), 128)] = half[:, 0:128].T
        trade.wait_send()

        @pl.when((gap >= 1) & (gap <= 7))
        def _():
            send_turn.wait_send()

    @pl.when(gap >= 9)
    def _():
        send_turn.wait_recv()
        tile_ref[...] = half[...]

    flop_in.wait_recv()
    for kk in range(2):
        for i in range(2):
            r = i * 256 + kk * 128
            gb_ref[r : r + 128, :] = flip[kk, i]

    for c in sent:
        c.wait_send()
    to_core.wait_send()
    swap.wait_send()
    flop.wait_send()

    @pl.when(a != b)
    def _():
        send_flip.wait_send()

    @pl.when(a < 2)
    def _():
        @pl.loop(1, 16)
        def _(i):
            spread(i).wait_send()

    @pl.loop(1, 16)
    def _(i):
        rs(i).wait_send()
        ag(i).wait_send()

    @pl.loop(0, 9)
    def _(d):
        to, c = tile(d)

        @pl.when(to != b)
        def _():
            c.wait_send()


def gram_parts(x_slab):
    vmem = pl.BlockSpec(memory_space=pltpu.VMEM)
    dma = pltpu.SemaphoreType.DMA
    shapes = [(128, 256), (512, 256), (512, 256), (512, 512), (8, 256)]
    return pl.pallas_call(
        gram_kernel,
        out_shape=[jax.ShapeDtypeStruct(s, F32) for s in shapes],
        in_specs=[vmem],
        out_specs=[vmem] * 5,
        scratch_shapes=[
            pltpu.VMEM((16, 512, 128), F32),
            pltpu.VMEM((512, 128), F32),
            pltpu.VMEM((512, 256), F32),
            pltpu.VMEM((16, 128, 256), F32),
            pltpu.VMEM((16, 24, 256), F32),
            pltpu.VMEM((16, 24, 256), F32),
            pltpu.VMEM((48, 256), F32),
            pltpu.VMEM((16, 48, 256), F32),
            pltpu.VMEM((2, 3, 2, 128, 256), F32),
            pltpu.VMEM((2, 2, 128, 256), F32),
            pltpu.VMEM((16, 128, 256), F32),
            pltpu.VMEM((128, 256), F32),
            pltpu.VMEM((128, 256), F32),
            pltpu.VMEM((8, 256), F32),
            dma((20,)), dma((16,)),
            dma((5,)), dma((5,)),
            dma((16,)), dma((16,)),
            dma((16,)), dma((2,)),
            dma((16,)), dma((16,)),
            dma((9,)), dma((16,)),
            dma((2,)), dma((2,)),
        ],
        compiler_params=pltpu.CompilerParams(
            collective_id=0, has_side_effects=True, vmem_limit_bytes=40 * 1024 * 1024
        ),
        name="gram_parts",
    )(x_slab)


def product(left, right):
    return jnp.dot(left, right, preferred_element_type=F32, precision=HIGH)


def invert_lower(block):
    factor = jnp.linalg.cholesky(block)
    identity = jnp.eye(block.shape[0], dtype=block.dtype)
    return lax.linalg.triangular_solve(factor, identity, left_side=True, lower=True)


def on_device(x_slab, weight_c):
    x, y, k, z, h = place()
    a = x * 8 + y
    b = z * 2 + h
    tile, ga, gb, diag, sq = gram_parts(x_slab)
    squares = jnp.sum(sq)
    factor_c = weight_c[0] / squares
    rows = a * 256 + k * 128 + jnp.arange(128, dtype=jnp.int32)
    cols = b * 256 + jnp.arange(256, dtype=jnp.int32)
    ids = jnp.concatenate([rows, cols])
    first = jnp.arange(512, dtype=jnp.int32)
    both = jnp.concatenate([lax.dynamic_slice_in_dim(ga, k * 128, 128, 1), gb], axis=1)
    both = both * factor_c + (first[:, None] == ids[None, :]).astype(F32)
    diag = diag * factor_c + jnp.eye(512, dtype=F32)
    gram = tile * factor_c + (rows[:, None] == cols[None, :]).astype(F32)
    inv1 = invert_lower(diag[:256, :256])
    cross = product(diag[256:, :256], inv1.T)
    inv2 = invert_lower(diag[256:, 256:] - product(cross, cross.T))
    low1 = product(inv1, both[:256])
    low1 = jnp.where(ids[None, :] >= first[:256, None], low1, 0.0)
    low2 = product(inv2, both[256:] - product(cross, low1))
    low2 = jnp.where(ids[None, :] >= first[256:, None], low2, 0.0)
    low = jnp.concatenate([low1, low2], axis=0)
    out = gram - lax.dot_general(
        low[:, :128], low[:, 128:], (((0,), (0,)), ((), ())), precision=HIGH, preferred_element_type=F32
    )
    return out, low[:, :128].T, jnp.stack([inv1, inv2]), jnp.sqrt(squares).reshape(1)


def solution(mesh):
    split = Mesh(mesh.devices.reshape(2, 8, 2, 8, 2), AXES)
    return jax.shard_map(
        on_device, mesh=split, in_specs=(P(COL, ROW), P()),
        out_specs=(P(ROW, COL), P(ROW, None), P(), P()), check_vma=False,
    )
```

time: 584 us -> 332 us (0.57)
  the two profiles are of different devices: /device:TPU:1 before, /device:TPU:57 now
where the time goes in v1:
time: 332 us
  Pallas kernels  197 us (59%)
  other arithmetic  110 us (33%)
  local copies, waits for them, and re-layouts  10.5 us (3%)
  between operations  6.84 us (2%)
  matrix products  6.75 us (2%)
    pallas_call x1, Pallas kernels, gram_parts(): pl.pallas_call(gram_kernel, out_shape=[jax.ShapeDtypeStruct(s, F32) for s...  197 us
    another operation x13, other arithmetic, invert_lower(): factor = jnp.linalg.cholesky(block)  68.5 us
    another operation x5, other arithmetic, invert_lower(): lax.linalg.triangular_solve(factor, identity, left_side=True, lower=True)  39.8 us
    another operation x15, local copies, waits for them, and re-layouts, invert_lower(): lax.linalg.triangular_solve(factor, identity, left_side=True, lower=True)  7.99 us

profile of v1, /device:TPU:57, one launch (start us, length us, event | category | flops | bytes accessed | tf_op | source)
XLA Modules:
  0.0 331.6 jit_solution(3196778298507392460)
XLA Ops:
  0.6 0.9 copy-done
  1.6 197.2 %gram_parts.1 = (f32[128,256]{1,0:T(8,128)S(1)}, f32[512,256]{1,0:T(8,128)S(1)}, f32[512,256]{1,0:T(8,128)S(1)}, f32[512,512]{1,0:T(8,128)S(1)}, f32[8,256]{1,0:T(8,128)S(1)}) custom-call(f32[512,128]{1,0:T(8,128)S(1)} %copy-done), custom_call_target="tpu_custom_call" | custom-call | tf_op jit(solution)/shard_map/gram_parts/pallas_call | solution.py:341
  198.8 0.7 reduce_sum.9
  201.5 11.7 %cholesky.130 = f32[128,128]{1,0:T(8,128)S(1)} custom-call(f32[128,128]{1,0:T(8,128)S(1)} %cholesky.194), custom_call_target="Cholesky" | custom-call | tf_op jit(solution)/shard_map/jit(cholesky)/cholesky | solution.py:381
  213.3 9.8 %custom-call.13 = f32[1,128,128]{1,2,0:T(8,128)S(1)} custom-call(f32[1,128,128]{2,1,0:T(8,128)S(1)} %get-tuple-element.63), custom_call_target="InvertDiagBlocksLowerTriangular" | custom-call | tf_op jit(solution)/shard_map/jit(cholesky)/cholesky | solution.py:381
  223.6 11.7 %cholesky.147 = f32[128,128]{1,0:T(8,128)S(1)} custom-call(f32[128,128]{1,0:T(8,128)S(1)} %convolution_subtract_fusion.6), custom_call_target="Cholesky" | custom-call | tf_op jit(solution)/shard_map/jit(cholesky)/cholesky | solution.py:381
  235.3 0.6 compare_reduce_fusion.2
  237.4 4.0 %while.4 = (s32[]{:T(128)}, f32[256,256]{1,0:T(8,128)S(1)}, s32[2,2]{1,0:T(2,128)S(1)}, f32[2,128,128]{2,1,0:T(8,128)S(1)}, s32[]{:T(128)}) while((s32[]{:T(128)}, f32[256,256]{1,0:T(8,128)S(1)}, s32[2,2]{1,0:T(2,128)S(1)}, f32[2,128,128]{2,1,0:T(8,128)S(1)}, s32[]{:T(128)}) %tuple.48), condition=%wide.while_cond, body=%wide.while_body.sunk | while | flops 2 | bytes 131181 | solution.py:383
  237.4 0.6 fusion.46
  238.0 1.4 bitcast_dynamic-update-slice_fusion.4
  239.4 0.6 fusion.46
  240.0 1.4 bitcast_dynamic-update-slice_fusion.4
  241.4 19.9 %custom-call.14 = f32[2,128,128]{1,2,0:T(8,128)S(1)} custom-call(f32[2,128,128]{2,1,0:T(8,128)S(1)} %get-tuple-element.30), custom_call_target="InvertDiagBlocksLowerTriangular" | custom-call | tf_op jit(solution)/shard_map/triangular_solve/custom-call.0 | solution.py:383
  262.3 0.6 fusion.4
  262.9 0.4 convolution_subtract_fusion.1
  263.5 11.7 %cholesky.164 = f32[128,128]{1,0:T(8,128)S(1)} custom-call(f32[128,128]{1,0:T(8,128)S(1)} %cholesky.197), custom_call_target="Cholesky" | custom-call | tf_op jit(solution)/shard_map/jit(cholesky)/cholesky | solution.py:381
  275.2 9.8 %custom-call.15 = f32[1,128,128]{1,2,0:T(8,128)S(1)} custom-call(f32[1,128,128]{2,1,0:T(8,128)S(1)} %get-tuple-element.59), custom_call_target="InvertDiagBlocksLowerTriangular" | custom-call | tf_op jit(solution)/shard_map/jit(cholesky)/cholesky | solution.py:381
  285.5 11.7 %cholesky.181 = f32[128,128]{1,0:T(8,128)S(1)} custom-call(f32[128,128]{1,0:T(8,128)S(1)} %convolution_subtract_fusion.5), custom_call_target="Cholesky" | custom-call | tf_op jit(solution)/shard_map/jit(cholesky)/cholesky | solution.py:381
  297.3 0.6 compare_reduce_fusion
  297.9 0.6 compare_reduce_fusion.1
  299.9 4.0 %while.5 = (s32[]{:T(128)}, f32[256,256]{1,0:T(8,128)S(1)}, s32[2,2]{1,0:T(2,128)S(1)}, f32[2,128,128]{2,1,0:T(8,128)S(1)}, s32[]{:T(128)}) while((s32[]{:T(128)}, f32[256,256]{1,0:T(8,128)S(1)}, s32[2,2]{1,0:T(2,128)S(1)}, f32[2,128,128]{2,1,0:T(8,128)S(1)}, s32[]{:T(128)}) %tuple.54), condition=%wide.while_cond.clone, body=%wide.while_body.clone.sunk | while | flops 2 | bytes 131181 | solution.py:383
  299.9 0.6 fusion.47
  300.5 1.4 bitcast_dynamic-update-slice_fusion.5
  301.9 0.6 fusion.47
  302.5 1.4 bitcast_dynamic-update-slice_fusion.5
  303.9 19.9 %custom-call.16 = f32[2,128,128]{1,2,0:T(8,128)S(1)} custom-call(f32[2,128,128]{2,1,0:T(8,128)S(1)} %get-tuple-element.31), custom_call_target="InvertDiagBlocksLowerTriangular" | custom-call | tf_op jit(solution)/shard_map/triangular_solve/custom-call.0 | solution.py:383
  324.8 0.8 pad_maximum_fusion.2
  325.8 0.6 convolution_select_fusion.1
  326.4 0.6 convolution_subtract_fusion
  327.0 0.6 convolution_select_fusion
  327.7 0.8 copy.10
  328.5 1.3 convolution_subtract_fusion.2
  (49 shorter events, 4.2 us)
Async XLA Ops:
  0.6 1.0 copy-start

commit v2 on v1

--- a/solution.py
+++ b/solution.py
@@ -373,43 +373,158 @@
     )(x_slab)
 
 
-def product(left, right):
-    return jnp.dot(left, right, preferred_element_type=F32, precision=HIGH)
-
-
-def invert_lower(block):
-    factor = jnp.linalg.cholesky(block)
-    identity = jnp.eye(block.shape[0], dtype=block.dtype)
-    return lax.linalg.triangular_solve(factor, identity, left_side=True, lower=True)
+def eliminate(get, put, n=128, nb=8):
+    lane = lax.broadcasted_iota(jnp.int32, (8, n), 1)
+    sub = lax.broadcasted_iota(jnp.int32, (8, n), 0)
+    tiles = [get(t) for t in range(n // 8)]
+    for j0 in range(0, n, nb):
+        t0 = j0 // 8
+        tn = nb // 8
+        live = range(t0, n // 8)
+        cols = {}
+        for l in range(nb):
+            for t in live:
+                cols[l, t] = jnp.broadcast_to(tiles[t][:, j0 + l : j0 + l + 1], (8, n))
+        mult = {}
+        inv = []
+        for l in range(nb):
+            tl, rl = t0 + l // 8, l % 8
+            piv = jnp.broadcast_to(cols[l, tl][rl : rl + 1, :], (8, n))
+            r = 1.0 / piv
+            inv.append(piv)
+            for t in live:
+                if t < tl:
+                    continue
+                m = cols[l, t] * r
+                if t == tl:
+                    m = jnp.where(sub > rl, m, 0.0)
+                mult[l, t] = m
+            for q in range(l + 1, nb):
+                tq, rq = t0 + q // 8, q % 8
+                s = jnp.broadcast_to(cols[l, tq][rq : rq + 1, :], (8, n))
+                for t in live:
+                    if t < tq:
+                        continue
+                    cols[q, t] = cols[q, t] - mult[l, t] * s
+        rows = []
+        for l in range(nb):
+            tl, rl = t0 + l // 8, l % 8
+            piv_row = jnp.where(lane == j0 + l, 1.0, jnp.broadcast_to(tiles[tl][rl : rl + 1, :], (8, n)))
+            rows.append(piv_row)
+            for t in range(tl, t0 + tn):
+                keep = tiles[t]
+                if t == tl:
+                    zeroed = jnp.where((lane == j0 + l) & (sub > rl), 0.0, keep)
+                    tiles[t] = zeroed - mult[l, t] * piv_row
+                else:
+                    tiles[t] = jnp.where(lane == j0 + l, 0.0, keep) - mult[l, t] * piv_row
+            tiles[tl] = jnp.where((sub == rl), piv_row, tiles[tl])
+        inside = (lane >= j0) & (lane < j0 + nb)
+        masked = [jnp.where((lane > j0 + l) & (lane < j0 + nb), 0.0, rows[l]) for l in range(nb)]
+        for t in range(t0 + tn, n // 8):
+            acc = jnp.where(inside, 0.0, tiles[t])
+            for l in range(nb):
+                acc = acc - mult[l, t] * masked[l]
+            tiles[t] = acc
+        for l in range(nb):
+            tl, rl = t0 + l // 8, l % 8
+            tiles[tl] = jnp.where(sub == rl, tiles[tl] * lax.rsqrt(inv[l]), tiles[tl])
+        for t in range(t0, t0 + tn):
+            rr = sub + 8 * t
+            put(t, jnp.where(lane <= rr, tiles[t], 0.0))
+
+
+def dot(left, right, ca=1, cb=0):
+    return lax.dot_general(
+        left, right, (((ca,), (cb,)), ((), ())), precision=HIGH, preferred_element_type=F32
+    )
+
+
+def factor_pair(s, inv_ref, cross_ref, w):
+    def half():
+        def put(t, v):
+            w[8 * t : 8 * t + 8, :] = v
+
+        eliminate(lambda t: w[8 * t : 8 * t + 8, :], put)
+
+    @pl.loop(0, 2)
+    def _(p):
+        base = pl.multiple_of(p * 256, 256)
+        top, low = pl.ds(base, 128), pl.ds(base + 128, 128)
+        w[...] = s[top, top]
+        half()
+        i11 = w[...]
+        l21 = dot(s[low, top], i11, 1, 1)
+        w[...] = s[low, low] - dot(l21, l21, 1, 1)
+        half()
+        i22 = w[...]
+        inv_ref[p, 0:128, 0:128] = i11
+        inv_ref[p, 0:128, 128:256] = jnp.zeros((128, 128), F32)
+        inv_ref[p, 128:256, 128:256] = i22
+        inv_ref[p, 128:256, 0:128] = -dot(i22, dot(l21, i11))
+
+        @pl.when(p == 0)
+        def _():
+            c = dot(s[256:512, 0:256], inv_ref[0], 1, 1)
+            cross_ref[...] = c
+            s[256:512, 256:512] = s[256:512, 256:512] - dot(c, c, 1, 1)
+
+
+def finish_kernel(
+    weight_ref, tile_ref, ga_ref, gb_ref, d_ref, sq_ref, out_ref, pan_ref, inv_ref, fro_ref,
+    s, w, cross, g, low,
+):
+    x, y, k, z, h = place()
+    row0 = (x * 8 + y) * 256 + k * 128
+    col0 = (z * 2 + h) * 256
+    squares = jnp.sum(jnp.sum(sq_ref[...], axis=0, keepdims=True), axis=1, keepdims=True)
+    fro_ref[0] = jnp.sqrt(squares)[0, 0]
+    scale = weight_ref[0] / squares
+
+    def iota(shape, dim, start=0):
+        return lax.broadcasted_iota(jnp.int32, shape, dim) + start
+
+    def scaled(v, r0, c0):
+        eye = (iota(v.shape, 0, r0) == iota(v.shape, 1, c0)).astype(F32)
+        return v * scale + eye
+
+    s[...] = scaled(d_ref[...], 0, 0)
+    g[:, 0:128] = scaled(ga_ref[:, pl.ds(pl.multiple_of(k * 128, 128), 128)], 0, row0)
+    g[:, 128:384] = scaled(gb_ref[...], 0, col0)
+    factor_pair(s, inv_ref, cross, w)
+    lane = iota((256, 384), 1)
+    ids = lane + jnp.where(lane < 128, row0, col0 - 128)
+    first = iota((256, 384), 0)
+    one = jnp.where(ids >= first, dot(inv_ref[0], g[0:256, :]), 0.0)
+    low[0:256, :] = one
+    two = dot(inv_ref[1], g[256:512, :] - dot(cross[...], one))
+    low[256:512, :] = jnp.where(ids >= first + 256, two, 0.0)
+    out_ref[...] = scaled(tile_ref[...], row0, col0) - dot(low[:, 0:128], low[:, 128:384], 0, 0)
+    pan_ref[...] = low[:, 0:128].T
+
+
+def finish(weight_c, tile, ga, gb, diag, sq):
+    vmem, smem = pl.BlockSpec(memory_space=pltpu.VMEM), pl.BlockSpec(memory_space=pltpu.SMEM)
+    shapes = [(128, 256), (128, 512), (2, 256, 256), (1,)]
+    return pl.pallas_call(
+        finish_kernel,
+        out_shape=[jax.ShapeDtypeStruct(s, F32) for s in shapes],
+        in_specs=[smem] + [vmem] * 5,
+        out_specs=[vmem] * 3 + [smem],
+        scratch_shapes=[
+            pltpu.VMEM((512, 512), F32),
+            pltpu.VMEM((128, 128), F32),
+            pltpu.VMEM((256, 256), F32),
+            pltpu.VMEM((512, 384), F32),
+            pltpu.VMEM((512, 384), F32),
+        ],
+        compiler_params=pltpu.CompilerParams(vmem_limit_bytes=40 * 1024 * 1024),
+        name="finish",
+    )(weight_c, tile, ga, gb, diag, sq)
 
 
 def on_device(x_slab, weight_c):
-    x, y, k, z, h = place()
-    a = x * 8 + y
-    b = z * 2 + h
-    tile, ga, gb, diag, sq = gram_parts(x_slab)
-    squares = jnp.sum(sq)
-    factor_c = weight_c[0] / squares
-    rows = a * 256 + k * 128 + jnp.arange(128, dtype=jnp.int32)
-    cols = b * 256 + jnp.arange(256, dtype=jnp.int32)
-    ids = jnp.concatenate([rows, cols])
-    first = jnp.arange(512, dtype=jnp.int32)
-    both = jnp.concatenate([lax.dynamic_slice_in_dim(ga, k * 128, 128, 1), gb], axis=1)
-    both = both * factor_c + (first[:, None] == ids[None, :]).astype(F32)
-    diag = diag * factor_c + jnp.eye(512, dtype=F32)
-    gram = tile * factor_c + (rows[:, None] == cols[None, :]).astype(F32)
-    inv1 = invert_lower(diag[:256, :256])
-    cross = product(diag[256:, :256], inv1.T)
-    inv2 = invert_lower(diag[256:, 256:] - product(cross, cross.T))
-    low1 = product(inv1, both[:256])
-    low1 = jnp.where(ids[None, :] >= first[:256, None], low1, 0.0)
-    low2 = product(inv2, both[256:] - product(cross, low1))
-    low2 = jnp.where(ids[None, :] >= first[256:, None], low2, 0.0)
-    low = jnp.concatenate([low1, low2], axis=0)
-    out = gram - lax.dot_general(
-        low[:, :128], low[:, 128:], (((0,), (0,)), ((), ())), precision=HIGH, preferred_element_type=F32
-    )
-    return out, low[:, :128].T, jnp.stack([inv1, inv2]), jnp.sqrt(squares).reshape(1)
+    return finish(weight_c, *gram_parts(x_slab))
 
 
 def solution(mesh):

time: 332 us -> 222 us (0.67)
  other arithmetic: 110 us -> 0 us
  Pallas kernels: 197 us -> 220 us
  local copies, waits for them, and re-layouts: 10.5 us -> 0.94 us
  matrix products: 6.75 us -> 0 us
  between operations: 6.84 us -> 1.29 us
    another operation x21 -> x0, other arithmetic: 109 us -> none  [the longest x13 68.5 us: invert_lower(): factor = jnp.linalg.cholesky(block)]
    pallas_call x0 -> x1, Pallas kernels: none -> 22.6 us  [finish(): pl.pallas_call(finish_kernel, out_shape=[jax.ShapeDtypeStruct(s, F32) for...]
    another operation x19 -> x0, local copies, waits for them, and re-layouts: 8.05 us -> none  [the longest x15 7.99 us: invert_lower(): lax.linalg.triangular_solve(factor, identity, left_side=True, lower=True)]
    dot_general x6 -> x0, matrix products: 4.04 us -> none  [the longest x5 2.79 us: product(): return jnp.dot(left, right, preferred_element_type=F32, precision=HIGH)]
where the time goes in v2:
time: 222 us
  Pallas kernels  220 us (99%)
    pallas_call x1, Pallas kernels, gram_parts(): pl.pallas_call(gram_kernel, out_shape=[jax.ShapeDtypeStruct(s, F32) for s...  197 us
    pallas_call x1, Pallas kernels, finish(): pl.pallas_call(finish_kernel, out_shape=[jax.ShapeDtypeStruct(s, F32) for...  22.6 us

profile of v2, /device:TPU:57, one launch (start us, length us, event | category | flops | bytes accessed | tf_op | source)
XLA Modules:
  0.0 222.1 jit_solution(9276224221298395746)
XLA Ops:
  1.3 0.0 copy-start
  1.3 0.9 copy-done
  2.2 197.2 %gram_parts.1 = (f32[128,256]{1,0:T(8,128)S(1)}, f32[512,256]{1,0:T(8,128)S(1)}, f32[512,256]{1,0:T(8,128)S(1)}, f32[512,512]{1,0:T(8,128)S(1)}, f32[8,256]{1,0:T(8,128)S(1)}) custom-call(f32[512,128]{1,0:T(8,128)S(1)} %copy-done), custom_call_target="tpu_custom_call" | custom-call | tf_op jit(solution)/shard_map/gram_parts/pallas_call | solution.py:341
  199.4 22.6 %finish.1 = (f32[128,256]{1,0:T(8,128)}, f32[128,512]{1,0:T(8,128)}, f32[2,256,256]{2,1,0:T(8,128)}, f32[1]{0:T(128)}) custom-call(f32[1]{0:T(128)S(6)} %copy.6.weight_ref, f32[128,256]{1,0:T(8,128)S(1)} %get-tuple-element.9.tile_ref, f32[512,256]{1,0:T(8,128)S(1)} %get-tuple-element.10.ga_ref, f32[512,256]{1,0:T(8,128)S(1)} %get-tuple-element.11.gb_ref, ...), custom_call_target="tpu_custom_call" | custom-call | tf_op jit(solution)/shard_map/finish/pallas_call | solution.py:509
Async XLA Ops:
  1.3 1.0 copy-start

commit v3 on v0

v3 whole, which is shorter than its diff:
```python
import jax
import jax.numpy as jnp
from jax import lax
from jax.experimental import pallas as pl
from jax.experimental.pallas import tpu as pltpu
from jax.sharding import Mesh
from jax.sharding import PartitionSpec as P

AXES = ("x", "y", "core", "z", "h")
ROW = ("x", "y", "core")
COL = ("z", "h")
HIGH = lax.Precision.HIGHEST
F32 = jnp.float32


def place():
    x, y, k = lax.axis_index("x"), lax.axis_index("y"), lax.axis_index("core")
    z, h = lax.axis_index("z"), lax.axis_index("h")
    return x, y, k, z, h


def dot(left, right, ca=1, cb=0):
    return lax.dot_general(
        left, right, (((ca,), (cb,)), ((), ())), precision=HIGH, preferred_element_type=F32
    )


def eliminate(get, put, n=128, nb=8):
    lane = lax.broadcasted_iota(jnp.int32, (8, n), 1)
    sub = lax.broadcasted_iota(jnp.int32, (8, n), 0)
    tiles = [get(t) for t in range(n // 8)]
    for j0 in range(0, n, nb):
        t0 = j0 // 8
        tn = nb // 8
        live = range(t0, n // 8)
        cols = {}
        for l in range(nb):
            for t in live:
                cols[l, t] = jnp.broadcast_to(tiles[t][:, j0 + l : j0 + l + 1], (8, n))
        mult = {}
        inv = []
        for l in range(nb):
            tl, rl = t0 + l // 8, l % 8
            piv = jnp.broadcast_to(cols[l, tl][rl : rl + 1, :], (8, n))
            r = 1.0 / piv
            inv.append(piv)
            for t in live:
                if t < tl:
                    continue
                m = cols[l, t] * r
                if t == tl:
                    m = jnp.where(sub > rl, m, 0.0)
                mult[l, t] = m
            for q in range(l + 1, nb):
                tq, rq = t0 + q // 8, q % 8
                s = jnp.broadcast_to(cols[l, tq][rq : rq + 1, :], (8, n))
                for t in live:
                    if t < tq:
                        continue
                    cols[q, t] = cols[q, t] - mult[l, t] * s
        rows = []
        for l in range(nb):
            tl, rl = t0 + l // 8, l % 8
            piv_row = jnp.where(lane == j0 + l, 1.0, jnp.broadcast_to(tiles[tl][rl : rl + 1, :], (8, n)))
            rows.append(piv_row)
            for t in range(tl, t0 + tn):
                keep = tiles[t]
                if t == tl:
                    zeroed = jnp.where((lane == j0 + l) & (sub > rl), 0.0, keep)
                    tiles[t] = zeroed - mult[l, t] * piv_row
                else:
                    tiles[t] = jnp.where(lane == j0 + l, 0.0, keep) - mult[l, t] * piv_row
            tiles[tl] = jnp.where((sub == rl), piv_row, tiles[tl])
        inside = (lane >= j0) & (lane < j0 + nb)
        masked = [jnp.where((lane > j0 + l) & (lane < j0 + nb), 0.0, rows[l]) for l in range(nb)]
        for t in range(t0 + tn, n // 8):
            acc = jnp.where(inside, 0.0, tiles[t])
            for l in range(nb):
                acc = acc - mult[l, t] * masked[l]
            tiles[t] = acc
        for l in range(nb):
            tl, rl = t0 + l // 8, l % 8
            tiles[tl] = jnp.where(sub == rl, tiles[tl] * lax.rsqrt(inv[l]), tiles[tl])
        for t in range(t0, t0 + tn):
            rr = sub + 8 * t
            put(t, jnp.where(lane <= rr, tiles[t], 0.0))


def factor_pair(s, inv_ref, cross_ref, w, hooks):
    def half():
        def put(t, v):
            w[8 * t : 8 * t + 8, :] = v

        eliminate(lambda t: w[8 * t : 8 * t + 8, :], put)

    for p in range(2):
        top, low = slice(p * 256, p * 256 + 128), slice(p * 256 + 128, p * 256 + 256)
        w[...] = s[top, top]
        half()
        hooks[2 * p]()
        i11 = w[...]
        l21 = dot(s[low, top], i11, 1, 1)
        w[...] = s[low, low] - dot(l21, l21, 1, 1)
        half()
        hooks[2 * p + 1]()
        i22 = w[...]
        inv_ref[p, 0:128, 0:128] = i11
        inv_ref[p, 0:128, 128:256] = jnp.zeros((128, 128), F32)
        inv_ref[p, 128:256, 128:256] = i22
        inv_ref[p, 128:256, 0:128] = -dot(i22, dot(l21, i11))
        if p == 0:
            c = dot(s[256:512, 0:256], inv_ref[0], 1, 1)
            cross_ref[...] = c
            s[256:512, 256:512] = s[256:512, 256:512] - dot(c, c, 1, 1)


def step_kernel(
    weight_ref, x_ref, out_ref, pan_ref, inv_ref, fro_ref,
    xb, other, lhs, prod, dprod, dland, dpc, dring, pland, red, pring, gpiece, gring,
    pile, turned, half_in, sqv, sqp, sqb, sqo, s, w, cross, g, low,
    s_ring, r_ring, s_core, r_core, s_drs, r_drs, s_dpl, r_dpl, s_dag, r_dag,
    s_rs, r_rs, s_ag, r_ag, s_gpl, r_gpl, s_a2a, r_a2a, s_mir, r_mir, s_sqa, r_sqa, s_sqb, r_sqb,
):
    x, y, k, z, h = place()
    a = x * 8 + y
    b = z * 2 + h

    def at_a(i):
        return (lax.div(i, 8), lax.rem(i, 8), k, z, h)

    def at_b(i):
        return (x, y, k, lax.div(i, 2), lax.rem(i, 2))

    partner = (x, y, 1 - k, z, h)
    across = (1 - x, y, k, z, h)
    mirror = (lax.div(b, 8), lax.rem(b, 8), k, lax.div(a, 2), lax.rem(a, 2))

    def copy(src, dst, ssem, rsem, dev):
        return pltpu.make_async_remote_copy(
            src_ref=src, dst_ref=dst, send_sem=ssem, recv_sem=rsem,
            device_id=dev, device_id_type=pl.DeviceIdType.MESH,
        )

    def chosen(i, j):
        odd = lax.rem(i + j, 2)
        return (i == j) | ((i < j) & (odd == 1)) | ((i > j) & (odd == 0))

    mine = chosen(a, b)

    def others(me, fn):
        @pl.loop(1, 16)
        def _(i):
            fn(i, lax.rem(me + i, 16))

    barrier = pltpu.get_barrier_semaphore()

    def signal(dev):
        pl.semaphore_signal(barrier, inc=1, device_id=dev, device_id_type=pl.DeviceIdType.MESH)

    others(a, lambda i, to: signal(at_a(to)))
    others(b, lambda i, to: signal(at_b(to)))
    signal(partner)

    @pl.when(a != b)
    def _():
        signal(mirror)

    def squares_of(v):
        return jnp.sum((v * v).reshape(64, 8, 128), axis=0)

    sqv[0] = squares_of(x_ref[...])
    xb[a] = x_ref[...]

    @pl.when(a != b)
    def _():
        pl.semaphore_wait(barrier, 32)

    @pl.when(a == b)
    def _():
        pl.semaphore_wait(barrier, 31)

    def sq_a(i, to, frm=None):
        return copy(sqv.at[0], sqp.at[a if frm is None else frm], s_sqa.at[i], r_sqa.at[a if frm is None else frm], at_a(to))

    def sq_b(i, to, frm=None):
        return copy(sqv.at[1], sqb.at[b if frm is None else frm], s_sqb.at[i], r_sqb.at[b if frm is None else frm], at_b(to))

    others(a, lambda i, to: sq_a(i, to).start())
    sqp[a] = sqv[0]

    sgn = 1 - 2 * k

    def slot(far, dy):
        return (1 - x if far else x) * 8 + lax.rem(y + dy + 8, 8)

    def y_at(dy):
        return (x, lax.rem(y + dy + 8, 8), k, z, h)

    sent = []

    def go(who, to, src=None):
        n = len(sent)
        c = copy(xb.at[who] if src is None else src, xb.at[who], s_ring.at[n], r_ring.at[who], to)
        c.start()
        sent.append(c)

    def arrive(who):
        copy(xb.at[who], xb.at[who], s_ring.at[0], r_ring.at[who], across).wait_recv()

    go(a, y_at(1), x_ref)
    go(a, y_at(-1), x_ref)
    go(a, across, x_ref)
    to_core = copy(x_ref, other, s_core.at[0], r_core.at[0], partner)
    to_core.start()

    tiles = []

    def tile(n, who):
        return copy(prod.at[who], pile.at[b], s_a2a.at[n], r_a2a.at[b], at_b(who))

    def work(far, dy):
        who = slot(far, dy)
        n = len(tiles)
        tiles.append(who)

        @pl.when(chosen(a, who) | (who < 2))
        def _():
            prod[who] = dot(xb[who], lhs[...], 0, 0)

        @pl.when(chosen(a, who) & (who != b))
        def _():
            tile(n, who).start()

    def d_rs(i, to, frm=None):
        me = b if frm is None else frm
        rows = pl.ds(pl.multiple_of(lax.rem(to, 8) * 16, 16), 16)
        return copy(dprod.at[lax.div(to, 8), rows], dland.at[me], s_drs.at[i], r_drs.at[me], at_b(to))

    def d_pl(i, to, who):
        return copy(dpc.at[who], dpc.at[who], s_dpl.at[i], r_dpl.at[who], at_a(to))

    def d_ag(i, to, frm, n):
        return copy(dpc.at[0:n], dring.at[k, frm, 0:n], s_dag.at[i], r_dag.at[frm], at_b(to))

    def p_rs(i, to, frm=None):
        me = b if frm is None else frm
        rows = pl.ds(pl.multiple_of(lax.rem(to, 8) * 16, 16), 16)
        return copy(prod.at[lax.div(to, 8), rows], pland.at[me], s_rs.at[i], r_rs.at[me], at_b(to))

    def p_ag(i, to, frm=None):
        me = b if frm is None else frm
        return copy(red, pring.at[k, me], s_ag.at[i], r_ag.at[me], at_b(to))

    def g_pl(i, to, frm=None):
        me = a if frm is None else frm
        return copy(gpiece, gring.at[k, me], s_gpl.at[i], r_gpl.at[me], at_a(to))

    def own_rows(ref):
        return ref[lax.div(b, 8), pl.ds(pl.multiple_of(lax.rem(b, 8) * 16, 16), 16), :]

    def total_of(ref):
        v = ref[0]
        for i in range(1, 16):
            v = v + ref[i]
        return v

    arrive(slot(0, -1))
    go(slot(0, -1), y_at(1))
    go(slot(0, -1), across)
    arrive(slot(0, 1))
    go(slot(0, 1), y_at(-1))
    go(slot(0, 1), across)
    to_core.wait_recv()
    lhs[:, pl.ds(pl.multiple_of(k * 128, 128), 128)] = x_ref[...]
    lhs[:, pl.ds(pl.multiple_of((1 - k) * 128, 128), 128)] = other[...]

    @pl.when(a < 2)
    def _():
        @pl.loop(0, 2)
        def _(i):
            dprod[i] = dot(xb[i], lhs[...], 0, 0)

        others(b, lambda i, to: d_rs(i, to).start())
        dland[b] = own_rows(dprod)

    others(a, lambda i, frm: sq_a(i, a, frm).wait_recv())
    sqv[1] = total_of(sqp)
    others(b, lambda i, to: sq_b(i, to).start())
    sqb[b] = sqv[1]

    work(0, 0)
    work(0, -1)
    work(0, 1)
    arrive(slot(1, 0))
    work(1, 0)
    arrive(slot(0, -2))
    go(slot(0, -2), y_at(1))
    arrive(slot(0, 2))
    go(slot(0, 2), y_at(-1))

    @pl.when(a < 2)
    def _():
        others(b, lambda i, frm: d_rs(i, frm, frm).wait_recv())
        dpc[a] = total_of(dland)

        @pl.when((a == 0) | (b >= 8))
        def _():
            others(a, lambda i, to: d_pl(i, to, a).start())

    work(0, -2)
    work(0, 2)
    arrive(slot(1, -1))
    go(slot(1, -1), y_at(1))
    arrive(slot(1, 1))
    go(slot(1, 1), y_at(-1))
    work(1, -1)
    work(1, 1)

    @pl.when(a != 0)
    def _():
        d_pl(0, 0, 0).wait_recv()

    @pl.when((a != 1) & (b >= 8))
    def _():
        d_pl(0, 1, 1).wait_recv()

    @pl.when(b < 8)
    def _():
        others(b, lambda i, to: d_ag(i, to, b, 1).start())

    @pl.when(b >= 8)
    def _():
        others(b, lambda i, to: d_ag(i, to, b, 2).start())
        dring[k, b, 1] = dpc[1]

    dring[k, b, 0] = dpc[0]
    arrive(slot(0, -3))
    arrive(slot(0, 3))
    go(slot(0, -3 * sgn), y_at(sgn))
    work(0, -3)
    work(0, 3)
    arrive(slot(1, -2))
    go(slot(1, -2), y_at(1))
    arrive(slot(1, 2))
    go(slot(1, 2), y_at(-1))
    work(1, -2)
    work(1, 2)
    arrive(slot(1, -3))
    arrive(slot(1, 3))
    go(slot(1, -3 * sgn), y_at(sgn))
    work(1, -3)
    work(1, 3)
    arrive(slot(0, 4))
    work(0, 4)
    arrive(slot(1, 4))
    work(1, 4)

    others(b, lambda i, to: p_rs(i, to).start())
    pland[b] = own_rows(prod)

    others(b, lambda i, frm: sq_b(i, b, frm).wait_recv())
    sqv[2] = total_of(sqb)
    sq_swap = copy(sqv.at[2], sqo, s_core.at[1], r_core.at[1], partner)
    sq_swap.start()

    @pl.loop(0, 8)
    def _(p):
        @pl.when(p != b)
        def _():
            d_ag(0, b, p, 1).wait_recv()

        @pl.when(p + 8 != b)
        def _():
            d_ag(0, b, p + 8, 2).wait_recv()

    d_swap = copy(dring.at[k], dring.at[k], s_core.at[2], r_core.at[2], partner)
    d_swap.start()
    sq_swap.wait_recv()
    both = sqv[2] + sqo[...]
    squares = jnp.sum(jnp.sum(both, axis=0, keepdims=True), axis=1, keepdims=True)
    fro_ref[0] = jnp.sqrt(squares)[0, 0]
    scale = weight_ref[0] / squares
    row0 = a * 256 + k * 128
    col0 = b * 256

    def iota(shape, dim, start=0):
        return lax.broadcasted_iota(jnp.int32, shape, dim) + start

    def scaled(v, r0, c0):
        eye = (iota(v.shape, 0, r0) == iota(v.shape, 1, c0)).astype(F32)
        return v * scale + eye

    copy(dring.at[1 - k], dring.at[1 - k], s_core.at[2], r_core.at[2], partner).wait_recv()
    for kk in range(2):
        for i in range(2):
            r = i * 256 + kk * 128
            for j in range(i + 1):
                v = dring[kk, 8 * i : 8 * i + 8, j].reshape(128, 256)
                s[r : r + 128, 256 * j : 256 * j + 256] = scaled(v, r, 256 * j)

    to_mirror = copy(red, gpiece, s_mir.at[0], r_mir.at[0], mirror)
    turn = copy(turned, half_in, s_mir.at[1], r_mir.at[1], mirror)
    trade = copy(
        turned.at[:, pl.ds(pl.multiple_of((1 - k) * 128, 128), 128)],
        half_in.at[:, 0:128],
        s_core.at[3], r_core.at[3], partner,
    )

    def hook_rows():
        others(b, lambda i, frm: p_rs(i, frm, frm).wait_recv())
        red[...] = total_of(pland)

        @pl.when(a != b)
        def _():
            to_mirror.start()

        others(b, lambda i, to: p_ag(i, to).start())
        pring[k, b] = red[...]

        @pl.when(a == b)
        def _():
            gpiece[...] = red[...]

    def hook_tile():
        @pl.when(mine)
        def _():
            pile[b] = prod[b]
            others(b, lambda i, frm: copy(prod.at[frm], pile.at[frm], s_a2a.at[0], r_a2a.at[frm], at_b(frm)).wait_recv())
            turned[...] = total_of(pile)
            trade.start()

            @pl.when(a != b)
            def _():
                turn.start()

    def hook_mirror():
        @pl.when(a != b)
        def _():
            to_mirror.wait_recv()

        others(a, lambda i, to: g_pl(i, to).start())
        gring[k, a] = gpiece[...]

    p_swap = copy(pring.at[k], pring.at[k], s_core.at[4], r_core.at[4], partner)
    g_swap = copy(gring.at[k], gring.at[k], s_core.at[5], r_core.at[5], partner)

    def hook_last():
        others(b, lambda i, frm: p_ag(i, b, frm).wait_recv())
        p_swap.start()

    factor_pair(s, inv_ref, cross, w, [hook_rows, hook_tile, hook_mirror, hook_last])

    others(a, lambda i, frm: g_pl(i, a, frm).wait_recv())
    g_swap.start()

    copy(pring.at[1 - k], pring.at[1 - k], s_core.at[4], r_core.at[4], partner).wait_recv()
    copy(gring.at[1 - k], gring.at[1 - k], s_core.at[5], r_core.at[5], partner).wait_recv()
    for kk in range(2):
        for i in range(2):
            r = i * 256 + kk * 128
            v = pring[kk, 8 * i : 8 * i + 8, :, pl.ds(pl.multiple_of(k * 128, 128), 128)].reshape(128, 128)
            g[r : r + 128, 0:128] = scaled(v, r, row0)
            v = gring[kk, 8 * i : 8 * i + 8].reshape(128, 256)
            g[r : r + 128, 128:384] = scaled(v, r, col0)

    lane = iota((256, 384), 1)
    ids = lane + jnp.where(lane < 128, row0, col0 - 128)
    first = iota((256, 384), 0)
    one = jnp.where(ids >= first, dot(inv_ref[0], g[0:256, :]), 0.0)
    low[0:256, :] = one
    two = dot(inv_ref[1], g[256:512, :] - dot(cross[...], one))
    low[256:512, :] = jnp.where(ids >= first + 256, two, 0.0)
    pan_ref[...] = low[:, 0:128].T
    less = dot(low[:, 0:128], low[:, 128:384], 0, 0)

    @pl.when(mine)
    def _():
        own = pl.ds(pl.multiple_of(k * 128, 128), 128)
        out_ref[:, own] = turned[:, own].T
        trade.wait_recv()
        out_ref[:, pl.ds(pl.multiple_of((1 - k) * 128, 128), 128)] = half_in[:, 0:128].T

    @pl.when(chosen(b, a) & (a != b))
    def _():
        turn.wait_recv()
        out_ref[...] = half_in[...]

    out_ref[...] = scaled(out_ref[...], row0, col0) - less

    for c in sent:
        c.wait_send()
    to_core.wait_send()
    sq_swap.wait_send()
    d_swap.wait_send()
    p_swap.wait_send()
    g_swap.wait_send()

    @pl.when(mine)
    def _():
        trade.wait_send()

    @pl.when(mine & (a != b))
    def _():
        turn.wait_send()

    @pl.when(a != b)
    def _():
        to_mirror.wait_send()

    @pl.when(a < 2)
    def _():
        others(b, lambda i, to: d_rs(i, to).wait_send())

    @pl.when((a == 0) | ((a == 1) & (b >= 8)))
    def _():
        others(a, lambda i, to: d_pl(i, to, a).wait_send())

    @pl.when(b < 8)
    def _():
        others(b, lambda i, to: d_ag(i, to, b, 1).wait_send())

    @pl.when(b >= 8)
    def _():
        others(b, lambda i, to: d_ag(i, to, b, 2).wait_send())

    others(a, lambda i, to: sq_a(i, to).wait_send())
    others(b, lambda i, to: sq_b(i, to).wait_send())
    others(b, lambda i, to: p_rs(i, to).wait_send())
    others(b, lambda i, to: p_ag(i, to).wait_send())
    others(a, lambda i, to: g_pl(i, to).wait_send())
    for n, who in enumerate(tiles):

        @pl.when(chosen(a, who) & (who != b))
        def _():
            tile(n, who).wait_send()


def on_device(x_slab, weight_c):
    vmem, smem = pl.BlockSpec(memory_space=pltpu.VMEM), pl.BlockSpec(memory_space=pltpu.SMEM)
    dma = pltpu.SemaphoreType.DMA
    shapes = [(128, 256), (128, 512), (2, 256, 256), (1,)]
    scratch = [
        (16, 512, 128), (512, 128), (512, 256), (16, 128, 256), (2, 128, 256), (16, 16, 256),
        (2, 16, 256), (2, 16, 2, 16, 256), (16, 16, 256), (16, 256), (2, 16, 16, 256), (16, 256),
        (2, 16, 16, 256), (16, 128, 256), (128, 256), (128, 256), (3, 8, 128), (16, 8, 128),
        (16, 8, 128), (8, 128), (512, 512), (128, 128), (256, 256), (512, 384), (512, 384),
    ]
    sems = [20, 16, 6, 6, 16, 16, 16, 2, 16, 16, 16, 16, 16, 16, 16, 16, 16, 16, 2, 2, 16, 16, 16, 16]
    return pl.pallas_call(
        step_kernel,
        out_shape=[jax.ShapeDtypeStruct(s, F32) for s in shapes],
        in_specs=[smem, vmem],
        out_specs=[vmem] * 3 + [smem],
        scratch_shapes=[pltpu.VMEM(s, F32) for s in scratch] + [dma((n,)) for n in sems],
        compiler_params=pltpu.CompilerParams(
            collective_id=0, has_side_effects=True, vmem_limit_bytes=48 * 1024 * 1024
        ),
        name="step",
    )(weight_c, x_slab)


def solution(mesh):
    split = Mesh(mesh.devices.reshape(2, 8, 2, 8, 2), AXES)
    return jax.shard_map(
        on_device, mesh=split, in_specs=(P(COL, ROW), P()),
        out_specs=(P(ROW, COL), P(ROW, None), P(), P()), check_vma=False,
    )
```

time: 584 us -> 137 us (0.23); the launches traced: 573 us -> 137 us
  waiting for transfers between devices: 284 us -> 0 us
  Pallas kernels: 0 us -> 131 us
  other arithmetic: 112 us -> 0 us
  blocking collectives: 104 us -> 0 us
  starting transfers between devices: 20.9 us -> 0 us
  matrix products: 18.1 us -> 0 us
  between operations: 20.3 us -> 3.06 us
  local copies, waits for them, and re-layouts: 14.1 us -> 3.1 us
    all_gather x3 -> x0, waiting for transfers between devices: 256 us -> none  [the longest x1 98.4 us: on_device(): lax.all_gather(x_slab, ROW, axis=1, tiled=True)]
    pallas_call x0 -> x1, Pallas kernels: none -> 131 us  [on_device(): pl.pallas_call(step_kernel, out_shape=[jax.ShapeDtypeStruct(s, F32) for s...]
    another operation x21 -> x0, other arithmetic: 109 us -> none  [the longest x13 68.8 us: invert_lower(): factor = jnp.linalg.cholesky(block)]
    psum x5 -> x0, blocking collectives: 60.7 us -> none  [by_axis(): x = lax.psum(x, axis)]
    all_to_all x2 -> x0, blocking collectives: 43.3 us -> none  [summed_on_arrival(): lax.all_to_all(blocks, axis, split_axis=0, concat_axis=0, tiled=True)]
    all_to_all x3 -> x0, waiting for transfers between devices: 27.1 us -> none  [the longest x2 27.1 us: from_everyone(): lax.all_to_all(jnp.broadcast_to(x[None], (size, *x.shape)), axis, 0, 0, t...]
    all_to_all x3 -> x0, starting transfers between devices: 20.8 us -> none  [the longest x2 11.2 us: from_everyone(): lax.all_to_all(jnp.broadcast_to(x[None], (size, *x.shape)), axis, 0, 0, t...]
    dot_general x9 -> x0, matrix products: 15.4 us -> none  [the longest x8 8.52 us: product(): jnp.dot(left, right, preferred_element_type=jnp.float32, precision=HIGH)]
  transfers between devices with their start and end apart: 6 -> 0, of which waited for: 5 -> 0; matrix products, arithmetic and copies ran while one was open for 0% -> 0% of each run, Pallas kernels for 0% -> 0%
where the time goes in v3:
time: 137 us
  Pallas kernels  131 us (96%)
  local copies, waits for them, and re-layouts  3.1 us (2%)
  between operations  3.06 us (2%)
    pallas_call x1, Pallas kernels, on_device(): pl.pallas_call(step_kernel, out_shape=[jax.ShapeDtypeStruct(s, F32) for s...  131 us
    unnamed x5, local copies, waits for them, and re-layouts  3.1 us

profile of v3, /device:TPU:1, one launch (start us, length us, event | category | flops | bytes accessed | tf_op | source)
XLA Modules:
  0.0 137.0 jit_solution(11499476882320365948)
XLA Ops:
  1.3 0.0 copy-start
  1.3 0.9 copy-done
  2.2 130.8 %step.1 = (f32[128,256]{1,0:T(8,128)S(1)}, f32[128,512]{1,0:T(8,128)S(1)}, f32[2,256,256]{2,1,0:T(8,128)S(1)}, f32[1]{0:T(128)}) custom-call(f32[1]{0:T(128)S(6)} %copy.10.weight_ref, f32[512,128]{1,0:T(8,128)S(1)} %copy-done), custom_call_target="tpu_custom_call" | custom-call | tf_op jit(solution)/shard_map/step/pallas_call | solution.py:549
  133.1 0.7 copy.11
  133.7 0.7 copy.12
  134.4 0.8 copy.13
Async XLA Ops:
  1.3 1.0 copy-start

commit v4 on v3

--- a/solution.py
+++ b/solution.py
@@ -25,11 +25,13 @@
     )
 
 
-def eliminate(get, put, n=128, nb=8):
+def eliminate(get, put, mid, n=128, nb=8):
     lane = lax.broadcasted_iota(jnp.int32, (8, n), 1)
     sub = lax.broadcasted_iota(jnp.int32, (8, n), 0)
     tiles = [get(t) for t in range(n // 8)]
     for j0 in range(0, n, nb):
+        if j0 == 64:
+            mid()
         t0 = j0 // 8
         tn = nb // 8
         live = range(t0, n // 8)
@@ -87,22 +89,22 @@
 
 
 def factor_pair(s, inv_ref, cross_ref, w, hooks):
-    def half():
+    def half(mid):
         def put(t, v):
             w[8 * t : 8 * t + 8, :] = v
 
-        eliminate(lambda t: w[8 * t : 8 * t + 8, :], put)
+        eliminate(lambda t: w[8 * t : 8 * t + 8, :], put, mid)
 
     for p in range(2):
         top, low = slice(p * 256, p * 256 + 128), slice(p * 256 + 128, p * 256 + 256)
         w[...] = s[top, top]
-        half()
-        hooks[2 * p]()
+        half(hooks[4 * p])
+        hooks[4 * p + 1]()
         i11 = w[...]
         l21 = dot(s[low, top], i11, 1, 1)
         w[...] = s[low, low] - dot(l21, l21, 1, 1)
-        half()
-        hooks[2 * p + 1]()
+        half(hooks[4 * p + 2])
+        hooks[4 * p + 3]()
         i22 = w[...]
         inv_ref[p, 0:128, 0:128] = i11
         inv_ref[p, 0:128, 128:256] = jnp.zeros((128, 128), F32)
@@ -117,9 +119,9 @@
 def step_kernel(
     weight_ref, x_ref, out_ref, pan_ref, inv_ref, fro_ref,
     xb, other, lhs, prod, dprod, dland, dpc, dring, pland, red, pring, gpiece, gring,
-    pile, turned, half_in, sqv, sqp, sqb, sqo, s, w, cross, g, low,
+    pile, part, hland, turned, half_in, sqv, sqp, sqb, sqo, s, w, cross, g, low,
     s_ring, r_ring, s_core, r_core, s_drs, r_drs, s_dpl, r_dpl, s_dag, r_dag,
-    s_rs, r_rs, s_ag, r_ag, s_gpl, r_gpl, s_a2a, r_a2a, s_mir, r_mir, s_sqa, r_sqa, s_sqb, r_sqb,
+    s_rs, r_rs, s_ag, r_ag, s_gpl, r_gpl, s_a2a, r_a2a, s_h, r_h, s_mir, r_mir, s_sqa, r_sqa, s_sqb, r_sqb,
 ):
     x, y, k, z, h = place()
     a = x * 8 + y
@@ -146,6 +148,8 @@
         return (i == j) | ((i < j) & (odd == 1)) | ((i > j) & (odd == 0))
 
     mine = chosen(a, b)
+    twin = z * 2 + 1 - h
+    helps = chosen(a, twin)
 
     def others(me, fn):
         @pl.loop(1, 16)
@@ -198,27 +202,57 @@
 
     sent = []
 
-    def go(who, to, src=None):
+    def part_of(ref, c):
+        return ref.at[256 * c : 256 * c + 256]
+
+    def go(who, c, to, src=None):
         n = len(sent)
-        c = copy(xb.at[who] if src is None else src, xb.at[who], s_ring.at[n], r_ring.at[who], to)
-        c.start()
-        sent.append(c)
-
-    def arrive(who):
-        copy(xb.at[who], xb.at[who], s_ring.at[0], r_ring.at[who], across).wait_recv()
-
-    go(a, y_at(1), x_ref)
-    go(a, y_at(-1), x_ref)
-    go(a, across, x_ref)
+        dst = part_of(xb.at[who], c)
+        d = copy(dst if src is None else part_of(src, c), dst, s_ring.at[n], r_ring.at[2 * who + c], to)
+        d.start()
+        sent.append(d)
+
+    def arrive(who, c):
+        dst = part_of(xb.at[who], c)
+        copy(dst, dst, s_ring.at[0], r_ring.at[2 * who + c], across).wait_recv()
+
+    def onward(far, dy, c, to_x=False, to_y=True):
+        for sign in (-1, 1):
+            who = slot(far, sign * dy)
+            arrive(who, c)
+            if to_y:
+                go(who, c, y_at(-sign))
+            if to_x:
+                go(who, c, across)
+
+    def last_hop(far, c):
+        arrive(slot(far, -3), c)
+        arrive(slot(far, 3), c)
+        go(slot(far, -3 * sgn), c, y_at(sgn))
+
+    for c in range(2):
+        go(a, c, y_at(1), x_ref)
+        go(a, c, y_at(-1), x_ref)
+        go(a, c, across, x_ref)
     to_core = copy(x_ref, other, s_core.at[0], r_core.at[0], partner)
     to_core.start()
 
     tiles = []
 
     def tile(n, who):
-        return copy(prod.at[who], pile.at[b], s_a2a.at[n], r_a2a.at[b], at_b(who))
-
-    def work(far, dy):
+        dest, side = lax.div(who, 2), lax.rem(who, 2)
+        return copy(
+            prod.at[who], pile.at[side, z], s_a2a.at[n], r_a2a.at[side * 8 + z], (x, y, k, dest, h)
+        )
+
+    held = []
+
+    def ship(n, who):
+        @pl.when(chosen(a, who) & (lax.div(who, 2) != z))
+        def _():
+            tile(n, who).start()
+
+    def work(far, dy, hold=False):
         who = slot(far, dy)
         n = len(tiles)
         tiles.append(who)
@@ -227,9 +261,10 @@
         def _():
             prod[who] = dot(xb[who], lhs[...], 0, 0)
 
-        @pl.when(chosen(a, who) & (who != b))
-        def _():
-            tile(n, who).start()
+        if hold:
+            held.append((n, who))
+        else:
+            ship(n, who)
 
     def d_rs(i, to, frm=None):
         me = b if frm is None else frm
@@ -264,12 +299,8 @@
             v = v + ref[i]
         return v
 
-    arrive(slot(0, -1))
-    go(slot(0, -1), y_at(1))
-    go(slot(0, -1), across)
-    arrive(slot(0, 1))
-    go(slot(0, 1), y_at(-1))
-    go(slot(0, 1), across)
+    onward(0, 1, 0, to_x=True)
+    onward(0, 1, 1, to_x=True)
     to_core.wait_recv()
     lhs[:, pl.ds(pl.multiple_of(k * 128, 128), 128)] = x_ref[...]
     lhs[:, pl.ds(pl.multiple_of((1 - k) * 128, 128), 128)] = other[...]
@@ -291,13 +322,19 @@
     work(0, 0)
     work(0, -1)
     work(0, 1)
-    arrive(slot(1, 0))
+    onward(0, 2, 0, to_x=True)
+    arrive(slot(1, 0), 0)
+    arrive(slot(1, 0), 1)
+    onward(0, 2, 1)
     work(1, 0)
-    arrive(slot(0, -2))
-    go(slot(0, -2), y_at(1))
-    arrive(slot(0, 2))
-    go(slot(0, 2), y_at(-1))
-
+    work(0, -2)
+    work(0, 2)
+    onward(1, 1, 0, to_y=False)
+    onward(1, 1, 1)
+    work(1, -1)
+    work(1, 1)
+    last_hop(0, 0)
+    last_hop(0, 1)
     @pl.when(a < 2)
     def _():
         others(b, lambda i, frm: d_rs(i, frm, frm).wait_recv())
@@ -307,15 +344,14 @@
         def _():
             others(a, lambda i, to: d_pl(i, to, a).start())
 
-    work(0, -2)
-    work(0, 2)
-    arrive(slot(1, -1))
-    go(slot(1, -1), y_at(1))
-    arrive(slot(1, 1))
-    go(slot(1, 1), y_at(-1))
-    work(1, -1)
-    work(1, 1)
-
+    work(0, -3, True)
+    work(0, 3, True)
+    onward(1, 2, 0)
+    onward(1, 2, 1)
+    work(1, -2, True)
+    work(1, 2, True)
+    last_hop(1, 0)
+    last_hop(1, 1)
     @pl.when(a != 0)
     def _():
         d_pl(0, 0, 0).wait_recv()
@@ -334,29 +370,19 @@
         dring[k, b, 1] = dpc[1]
 
     dring[k, b, 0] = dpc[0]
-    arrive(slot(0, -3))
-    arrive(slot(0, 3))
-    go(slot(0, -3 * sgn), y_at(sgn))
-    work(0, -3)
-    work(0, 3)
-    arrive(slot(1, -2))
-    go(slot(1, -2), y_at(1))
-    arrive(slot(1, 2))
-    go(slot(1, 2), y_at(-1))
-    work(1, -2)
-    work(1, 2)
-    arrive(slot(1, -3))
-    arrive(slot(1, 3))
-    go(slot(1, -3 * sgn), y_at(sgn))
-    work(1, -3)
-    work(1, 3)
-    arrive(slot(0, 4))
-    work(0, 4)
-    arrive(slot(1, 4))
-    work(1, 4)
+    arrive(slot(0, 4), 0)
+    arrive(slot(0, 4), 1)
+    work(0, 4, True)
+    work(1, -3, True)
+    work(1, 3, True)
+    arrive(slot(1, 4), 0)
+    arrive(slot(1, 4), 1)
+    work(1, 4, True)
 
     others(b, lambda i, to: p_rs(i, to).start())
     pland[b] = own_rows(prod)
+    for n, who in held:
+        ship(n, who)
 
     others(b, lambda i, frm: sq_b(i, b, frm).wait_recv())
     sqv[2] = total_of(sqb)
@@ -421,12 +447,39 @@
         def _():
             gpiece[...] = red[...]
 
+    to_twin = copy(part, hland, s_h.at[0], r_h.at[0], (x, y, k, z, 1 - h))
+
+    def sum_over_z(side, who):
+        pile[side, z] = prod[who]
+
+        @pl.loop(1, 8)
+        def _(i):
+            frm = lax.rem(z + i, 8)
+            copy(
+                prod.at[who], pile.at[side, frm], s_a2a.at[0], r_a2a.at[side * 8 + frm],
+                (x, y, k, frm, h),
+            ).wait_recv()
+
+        v = pile[side, 0]
+        for i in range(1, 8):
+            v = v + pile[side, i]
+        return v
+
+    def hook_half():
+        @pl.when(helps)
+        def _():
+            part[...] = sum_over_z(1 - h, twin)
+            to_twin.start()
+
+        @pl.when(mine)
+        def _():
+            turned[...] = sum_over_z(h, b)
+
     def hook_tile():
         @pl.when(mine)
         def _():
-            pile[b] = prod[b]
-            others(b, lambda i, frm: copy(prod.at[frm], pile.at[frm], s_a2a.at[0], r_a2a.at[frm], at_b(frm)).wait_recv())
-            turned[...] = total_of(pile)
+            to_twin.wait_recv()
+            turned[...] = turned[...] + hland[...]
             trade.start()
 
             @pl.when(a != b)
@@ -448,10 +501,17 @@
         others(b, lambda i, frm: p_ag(i, b, frm).wait_recv())
         p_swap.start()
 
-    factor_pair(s, inv_ref, cross, w, [hook_rows, hook_tile, hook_mirror, hook_last])
-
-    others(a, lambda i, frm: g_pl(i, a, frm).wait_recv())
-    g_swap.start()
+    def hook_rest():
+        others(a, lambda i, frm: g_pl(i, a, frm).wait_recv())
+        g_swap.start()
+
+    def idle():
+        pass
+
+    factor_pair(
+        s, inv_ref, cross, w,
+        [idle, idle, hook_rows, hook_half, hook_mirror, hook_tile, hook_last, hook_rest],
+    )
 
     copy(pring.at[1 - k], pring.at[1 - k], s_core.at[4], r_core.at[4], partner).wait_recv()
     copy(gring.at[1 - k], gring.at[1 - k], s_core.at[5], r_core.at[5], partner).wait_recv()
@@ -503,6 +563,10 @@
     def _():
         turn.wait_send()
 
+    @pl.when(helps)
+    def _():
+        to_twin.wait_send()
+
     @pl.when(a != b)
     def _():
         to_mirror.wait_send()
@@ -530,7 +594,7 @@
     others(a, lambda i, to: g_pl(i, to).wait_send())
     for n, who in enumerate(tiles):
 
-        @pl.when(chosen(a, who) & (who != b))
+        @pl.when(chosen(a, who) & (lax.div(who, 2) != z))
         def _():
             tile(n, who).wait_send()
 
@@ -542,10 +606,10 @@
     scratch = [
         (16, 512, 128), (512, 128), (512, 256), (16, 128, 256), (2, 128, 256), (16, 16, 256),
         (2, 16, 256), (2, 16, 2, 16, 256), (16, 16, 256), (16, 256), (2, 16, 16, 256), (16, 256),
-        (2, 16, 16, 256), (16, 128, 256), (128, 256), (128, 256), (3, 8, 128), (16, 8, 128),
+        (2, 16, 16, 256), (2, 8, 128, 256), (128, 256), (128, 256), (128, 256), (128, 256), (3, 8, 128), (16, 8, 128),
         (16, 8, 128), (8, 128), (512, 512), (128, 128), (256, 256), (512, 384), (512, 384),
     ]
-    sems = [20, 16, 6, 6, 16, 16, 16, 2, 16, 16, 16, 16, 16, 16, 16, 16, 16, 16, 2, 2, 16, 16, 16, 16]
+    sems = [40, 32, 6, 6, 16, 16, 16, 2, 16, 16, 16, 16, 16, 16, 16, 16, 16, 16, 1, 1, 2, 2, 16, 16, 16, 16]
     return pl.pallas_call(
         step_kernel,
         out_shape=[jax.ShapeDtypeStruct(s, F32) for s in shapes],

time: 137 us -> 120 us (0.88)
  Pallas kernels: 131 us -> 114 us
    pallas_call x1, Pallas kernels: 131 us -> 114 us  [on_device(): pl.pallas_call(step_kernel, out_shape=[jax.ShapeDtypeStruct(s, F32) for s...]
where the time goes in v4:
time: 120 us
  Pallas kernels  114 us (95%)
  local copies, waits for them, and re-layouts  3.1 us (3%)
  between operations  3.06 us (3%)
    pallas_call x1, Pallas kernels, on_device(): pl.pallas_call(step_kernel, out_shape=[jax.ShapeDtypeStruct(s, F32) for s...  114 us
    unnamed x5, local copies, waits for them, and re-layouts  3.1 us

profile of v4, /device:TPU:1, one launch (start us, length us, event | category | flops | bytes accessed | tf_op | source)
XLA Modules:
  0.0 120.0 jit_solution(11868550087815404460)
XLA Ops:
  1.3 0.0 copy-start
  1.3 0.9 copy-done
  2.2 113.9 %step.1 = (f32[128,256]{1,0:T(8,128)S(1)}, f32[128,512]{1,0:T(8,128)S(1)}, f32[2,256,256]{2,1,0:T(8,128)S(1)}, f32[1]{0:T(128)}) custom-call(f32[1]{0:T(128)S(6)} %copy.10.weight_ref, f32[512,128]{1,0:T(8,128)S(1)} %copy-done), custom_call_target="tpu_custom_call" | custom-call | tf_op jit(solution)/shard_map/step/pallas_call | solution.py:613
  116.1 0.7 copy.11
  116.8 0.7 copy.12
  117.5 0.8 copy.13
Async XLA Ops:
  1.3 1.0 copy-start

commit v5 on v4

--- a/solution.py
+++ b/solution.py
@@ -252,19 +252,21 @@
         def _():
             tile(n, who).start()
 
+    def multiply(n, who):
+        @pl.when(chosen(a, who))
+        def _():
+            prod[who] = dot(xb[who], lhs[...], 0, 0)
+
+        ship(n, who)
+
     def work(far, dy, hold=False):
         who = slot(far, dy)
         n = len(tiles)
         tiles.append(who)
-
-        @pl.when(chosen(a, who) | (who < 2))
-        def _():
-            prod[who] = dot(xb[who], lhs[...], 0, 0)
-
         if hold:
             held.append((n, who))
         else:
-            ship(n, who)
+            multiply(n, who)
 
     def d_rs(i, to, frm=None):
         me = b if frm is None else frm
@@ -280,7 +282,7 @@
     def p_rs(i, to, frm=None):
         me = b if frm is None else frm
         rows = pl.ds(pl.multiple_of(lax.rem(to, 8) * 16, 16), 16)
-        return copy(prod.at[lax.div(to, 8), rows], pland.at[me], s_rs.at[i], r_rs.at[me], at_b(to))
+        return copy(dprod.at[lax.div(to, 8), rows], pland.at[me], s_rs.at[i], r_rs.at[me], at_b(to))
 
     def p_ag(i, to, frm=None):
         me = b if frm is None else frm
@@ -379,10 +381,16 @@
     arrive(slot(1, 4), 1)
     work(1, 4, True)
 
+    @pl.when(a >= 2)
+    def _():
+        @pl.loop(0, 2)
+        def _(i):
+            dprod[i] = dot(xb[i], lhs[...], 0, 0)
+
     others(b, lambda i, to: p_rs(i, to).start())
-    pland[b] = own_rows(prod)
+    pland[b] = own_rows(dprod)
     for n, who in held:
-        ship(n, who)
+        multiply(n, who)
 
     others(b, lambda i, frm: sq_b(i, b, frm).wait_recv())
     sqv[2] = total_of(sqb)

time: 120 us -> 120 us (level)
  no operation moved by 1% of the time
where the time goes in v5:
time: 120 us
  Pallas kernels  114 us (95%)
  local copies, waits for them, and re-layouts  3.1 us (3%)
  between operations  3.06 us (3%)
    pallas_call x1, Pallas kernels, on_device(): pl.pallas_call(step_kernel, out_shape=[jax.ShapeDtypeStruct(s, F32) for s...  114 us
    unnamed x5, local copies, waits for them, and re-layouts  3.1 us

profile of v5, /device:TPU:1, one launch (start us, length us, event | category | flops | bytes accessed | tf_op | source)
XLA Modules:
  0.0 119.9 jit_solution(7029129350251615488)
XLA Ops:
  1.3 0.0 copy-start
  1.3 0.9 copy-done
  2.2 113.8 %step.1 = (f32[128,256]{1,0:T(8,128)S(1)}, f32[128,512]{1,0:T(8,128)S(1)}, f32[2,256,256]{2,1,0:T(8,128)S(1)}, f32[1]{0:T(128)}) custom-call(f32[1]{0:T(128)S(6)} %copy.10.weight_ref, f32[512,128]{1,0:T(8,128)S(1)} %copy-done), custom_call_target="tpu_custom_call" | custom-call | tf_op jit(solution)/shard_map/step/pallas_call | solution.py:621
  116.0 0.7 copy.11
  116.7 0.7 copy.12
  117.4 0.8 copy.13
Async XLA Ops:
  1.3 1.0 copy-start
